TPU v7x, 512 devices: a whole 4x4x16 slice. The times are simulated.
512 devices in a mesh: sym: 8 (over y, core), tile: 64 (over z, x).
Axes of the slice: x: 4, y: 4, z: 16, core: 2. Of those that a mesh axis runs over, the one named last changes fastest.
Arguments:
- amplitudes: bfloat16 [256, 131072], P(None, ('sym', 'tile')), may hold values from -6 to 6
- slot_cols: int32 [1024, 64], P(('sym', 'tile')), may hold values from 0 to 127, as said below
- slot_count: int32 [1024], P(('sym', 'tile')), may hold values from 16 to 64, as said below
- integrals: bfloat16 [1024, 64, 128, 128], P(('sym', 'tile')), may hold values from -0.0625 to 0.0625
- cycle_same: bfloat16 [8, 128, 128], P('sym'), may hold values from -0.375 to 0.375
- cycle_cross: bfloat16 [8, 128, 128], P('sym'), may hold values from -0.375 to 0.375
Outputs:
- residual: bfloat16 [256, 131072], P(None, ('sym', 'tile'))
Inputs may be any that keep to these rules, and one draw needn't show every extreme that they name: `slot_cols`: tile index within the symmetry block; the live entries of a row are distinct and rising. `slot_count`: some virtual-pair tile has all 64 slots live.
All inputs are finite; a program needn't handle non-finite values.
Results may differ from a plain program's by a relative error of at most 0.0044.
Values may be sent and summed in bfloat16 or wider, within the bound.
A program may use at most 128 MiB of HBM per device.

v0:
```python
import jax
import jax.numpy as jnp
from jax import lax
from jax.sharding import PartitionSpec as P


def from_partner(value, axis, bit):
    mask = 2**bit
    pairs = [(source, source ^ mask) for source in range(lax.axis_size(axis))]
    return lax.ppermute(value, axis, pairs)


def cycle_rows(same_rows, cross_rows, own_part, other_part, block_tiles, tile_width):
    items = own_part.shape[0]
    own_three = own_part.reshape(items, block_tiles, tile_width)
    other_three = other_part.reshape(items, block_tiles, tile_width)
    result = jnp.einsum("uv,pva->pua", same_rows, own_three, preferred_element_type=jnp.float32)
    result = result + jnp.einsum(
        "uv,pva->pua", cross_rows, other_three, preferred_element_type=jnp.float32
    )
    return result


def on_device(amplitudes, slot_cols, slot_count, integrals, cycle_same, cycle_cross):
    pair_count = amplitudes.shape[0]
    rows_local = integrals.shape[0]
    slot_total = integrals.shape[1]
    tile_width = integrals.shape[3]
    block_tiles = cycle_same.shape[1]
    gathered = lax.all_gather(amplitudes, "tile", axis=1, tiled=True)
    block_three = gathered.reshape(pair_count, block_tiles, tile_width)
    live_slot = lax.broadcasted_iota(jnp.int32, (rows_local, slot_total), 1) < slot_count[:, None]
    take_index = jnp.where(live_slot, slot_cols, block_tiles)
    ladder_parts = []
    for tile_row in range(rows_local):
        picked = jnp.take(block_three, take_index[tile_row], axis=1, mode="fill", fill_value=0)
        ladder_parts.append(
            jnp.einsum(
                "psc,sac->pa", picked, integrals[tile_row], preferred_element_type=jnp.float32
            )
        )
    ladder = jnp.stack(ladder_parts, axis=1).reshape(pair_count, rows_local * tile_width)
    dressed = (amplitudes.astype(jnp.float32) + ladder).astype(jnp.bfloat16)
    partner = from_partner(dressed, "sym", 0)
    whole_own, whole_partner = (
        lax.all_gather(dressed, "tile", axis=1, tiled=True),
        lax.all_gather(partner, "tile", axis=1, tiled=True),
    )
    position = lax.axis_index("tile")
    same_rows = lax.dynamic_slice_in_dim(cycle_same[0], position * rows_local, rows_local, 0)
    cross_rows = lax.dynamic_slice_in_dim(cycle_cross[0], position * rows_local, rows_local, 0)
    cycle_term = cycle_rows(
        same_rows, cross_rows, whole_own, whole_partner, block_tiles, tile_width
    )
    cycle_term = cycle_term.reshape(pair_count, rows_local * tile_width)
    return (ladder + cycle_term).astype(jnp.bfloat16)


def solution(mesh):
    in_specs = (
        P(None, ("sym", "tile")),
        P(("sym", "tile"), None),
        P(("sym", "tile")),
        P(("sym", "tile"), None, None, None),
        P("sym", None, None),
        P("sym", None, None),
    )
    out_specs = P(None, ("sym", "tile"))
    return jax.shard_map(
        on_device, mesh=mesh, in_specs=in_specs, out_specs=out_specs, check_vma=False
    )
```

profile of v0, /device:TPU:8, one launch (start us, length us, event | category | flops | bytes accessed | tf_op | source)
XLA Modules:
  0.0 553.8 jit_solution(9314749196532757080)
XLA Ops:
  6.5 0.0 copy-start
  6.5 0.0 all-gather.4.cloned.1.call-start
  6.5 1.7 copy.11
  8.2 0.0 all-gather.4.cloned.1.call-update
  8.2 0.0 all-gather.6.cloned.1.call-start
  8.3 0.8 compare_select_fusion.2
  9.1 161.6 %all-gather.4.cloned.1.call-done = bf16[256,16384]{0,1:T(8,128)(2,1)} async-done(((bf16[256,256]{0,1:T(8,128)(2,1)}), bf16[256,16384]{0,1:T(8,128)(2,1)}) %all-gather.4.cloned.1.call-update) | async-done | bytes 8388624 | tf_op jit(solution)/shard_map/all_gather | solution.py:30
  170.7 12.0 %copy.12 = bf16[256,128,128]{2,0,1:T(8,128)(2,1)} copy(bf16[256,128,128]{0,2,1:T(8,128)(2,1)} %bitcast.58) | data formatting | bytes 16777216 | tf_op jit(solution)/shard_map/reshape | solution.py:31
  182.7 6.4 %gather_fusion.1 = bf16[64,256,128]{2,1,0:T(8,128)(2,1)} fusion(bf16[256,128,128]{2,0,1:T(8,128)(2,1)} %copy.12, s32[1024]{0:T(1024)S(1)} %get-tuple-element.12), kind=kCustom, calls=%fused_computation.1.clone | custom fusion | bytes 8388864 | tf_op jit(solution)/shard_map/jit(_take)/gather | solution.py:36
  189.1 6.4 %gather_fusion = bf16[64,256,128]{2,1,0:T(8,128)(2,1)} fusion(bf16[256,128,128]{2,0,1:T(8,128)(2,1)} %copy.12, s32[1024]{0:T(1024)S(1)} %get-tuple-element.13), kind=kCustom, calls=%fused_computation.clone | custom fusion | bytes 8388864 | tf_op jit(solution)/shard_map/jit(_take)/gather | solution.py:36
  195.5 0.0 copy-start.1
  195.5 0.0 copy-start.4
  195.5 4.6 fusion.14
  200.1 0.0 copy-done.1
  200.1 0.8 copy-done.4
  200.8 0.0 copy-start.2
  200.8 1.6 fusion.19
  202.4 0.1 copy.15
  202.6 0.0 copy-done.2
  202.6 0.7 add_convert_fusion
  203.3 0.0 all-gather.6.cloned.1.call-update
  203.3 0.0 all-gather.8.cloned.1.call-start
  203.3 1.9 collective-permute-start
  205.3 1.5 collective-permute-done
  206.8 0.0 copy-start.3
  206.8 0.6 copy-done.3
  207.4 0.0 all-gather.8.cloned.1.call-update
  207.5 159.4 %all-gather.6.cloned.1.call-done = bf16[256,16384]{1,0:T(8,128)(2,1)} async-done(((bf16[256,256]{1,0:T(8,128)(2,1)}), bf16[256,16384]{1,0:T(8,128)(2,1)}) %all-gather.6.cloned.1.call-update) | async-done | bytes 8388624 | tf_op jit(solution)/shard_map/all_gather | solution.py:46
  366.8 9.2 %copy.16 = bf16[32,8,128,128]{3,2,1,0:T(8,128)(2,1)} copy(bf16[32,8,128,128]{3,1,2,0:T(8,128)(2,1)} %bitcast.56) | data formatting | bytes 16777216
  376.0 0.0 copy-done
  376.0 4.6 fusion.26
  380.6 152.2 %all-gather.8.cloned.1.call-done = bf16[256,16384]{1,0:T(8,128)(2,1)} async-done(((bf16[256,256]{1,0:T(8,128)(2,1)}), bf16[256,16384]{1,0:T(8,128)(2,1)}) %all-gather.8.cloned.1.call-update) | async-done | bytes 8388624 | tf_op jit(solution)/shard_map/all_gather | solution.py:47
  532.8 9.2 %copy.17 = bf16[32,8,128,128]{3,2,1,0:T(8,128)(2,1)} copy(bf16[32,8,128,128]{3,1,2,0:T(8,128)(2,1)} %bitcast.57) | data formatting | bytes 16777216
  542.0 4.6 convolution_add_fusion
  546.6 0.7 fusion.24
  (3 shorter events, 0.0 us)
Async XLA Ops:
  6.5 369.5 %copy-start = (bf16[1,128,128]{2,1,0:T(8,128)(2,1)S(1)}, bf16[1,128,128]{2,1,0:T(8,128)(2,1)}, u32[]{:S(2)}) copy-start(bf16[1,128,128]{2,1,0:T(8,128)(2,1)} %param.12) | copy-start | bytes 98308
  6.5 164.1 %all-gather.4.cloned.1.call-start = ((), (), s32[]{:S(2)}) async-start(), calls=%async_computation | async-start | bytes 8519680 | tf_op jit(solution)/shard_map/all_gather | solution.py:30
  8.2 358.6 %all-gather.6.cloned.1.call-start = ((), (), s32[]{:S(2)}) async-start(), calls=%async_computation.1 | async-start | bytes 8519680 | tf_op jit(solution)/shard_map/all_gather | solution.py:46
  195.5 4.6 copy-start.1
  195.5 5.3 copy-start.4
  200.8 1.7 copy-start.2
  203.3 329.5 %all-gather.8.cloned.1.call-start = ((), (), s32[]{:S(2)}) async-start(), calls=%async_computation.2 | async-start | bytes 8519680 | tf_op jit(solution)/shard_map/all_gather | solution.py:47
  203.3 3.5 collective-permute-start
  206.8 0.6 copy-start.3
Sparse Core Ops, SparseCore 0:
  10.3 160.3 all-gather.3
  203.4 163.3 all-gather.5
  369.7 163.0 all-gather.7
where the time goes:
time: 554 us
  waiting for transfers between devices  475 us (86%)
  local copies, waits for them, and re-layouts  46.4 us (8%)
  matrix products  15.3 us (3%)
  between operations  13.2 us (2%)
    all_gather x1, waiting for transfers between devices, on_device(): gathered = lax.all_gather(amplitudes, 'tile', axis=1, tiled=True)  162 us
    all_gather x1, waiting for transfers between devices, on_device(): lax.all_gather(dressed, 'tile', axis=1, tiled=True)  159 us
    all_gather x1, waiting for transfers between devices, on_device(): lax.all_gather(partner, 'tile', axis=1, tiled=True)  152 us
    unnamed x13, local copies, waits for them, and re-layouts  21.5 us
    gather x2, local copies, waits for them, and re-layouts, on_device(): jnp.take(block_three, take_index[tile_row], axis=1, mode='fill', fill_val...  12.8 us
    reshape x1, local copies, waits for them, and re-layouts, on_device(): block_three = gathered.reshape(pair_count, block_tiles, tile_width)  12 us
  transfers between devices with their start and end apart: 4, of which 4 were waited for; matrix products, arithmetic and copies ran while one was open for 3% of the time, Pallas kernels for 0%

commit v1 on v0

--- a/solution.py
+++ b/solution.py
@@ -1,7 +1,19 @@
+import functools
 import jax
 import jax.numpy as jnp
 from jax import lax
 from jax.sharding import PartitionSpec as P
+
+
+def measure_limits(z, along_axis, along_dim):
+    carry = lax.axis_size(along_axis)
+    plain = jnp.stack([z] * carry)
+    row_out = lax.all_to_all(plain, along_axis, 0, 0)
+    n_now = jnp.concatenate(row_out, axis=along_dim)
+    return n_now
+
+
+_remake_runs = functools.partial(measure_limits, along_axis="tile", along_dim=1)
 
 
 def from_partner(value, axis, bit):
@@ -43,7 +55,7 @@
     dressed = (amplitudes.astype(jnp.float32) + ladder).astype(jnp.bfloat16)
     partner = from_partner(dressed, "sym", 0)
     whole_own, whole_partner = (
-        lax.all_gather(dressed, "tile", axis=1, tiled=True),
+        _remake_runs(dressed),
         lax.all_gather(partner, "tile", axis=1, tiled=True),
     )
     position = lax.axis_index("tile")

time: 554 us -> 685 us (1.24)
  the two profiles are of different devices: /device:TPU:8 before, /device:TPU:68 now
where the time goes in v1:
time: 685 us
  waiting for transfers between devices  575 us (84%)
  local copies, waits for them, and re-layouts  65.7 us (10%)
  matrix products  15.3 us (2%)
  starting transfers between devices  13.6 us (2%)
  between operations  13.5 us (2%)
    all_gather x1, waiting for transfers between devices, on_device(): lax.all_gather(partner, 'tile', axis=1, tiled=True)  415 us
    all_gather x1, waiting for transfers between devices, on_device(): gathered = lax.all_gather(amplitudes, 'tile', axis=1, tiled=True)  159 us
  transfers between devices with their start and end apart: 4, of which 3 were waited for; matrix products, arithmetic and copies ran while one was open for 1% of the time, Pallas kernels for 0%

profile of v1, /device:TPU:68, one launch (start us, length us, event | category | flops | bytes accessed | tf_op | source)
XLA Modules:
  0.0 684.5 jit_solution(16179702592387552782)
XLA Ops:
  6.5 0.0 copy-start
  6.5 0.0 all-gather.3.cloned.1.call-start
  6.5 1.7 copy.16
  8.2 0.0 all-gather.3.cloned.1.call-update
  8.2 0.8 compare_select_fusion.2
  9.0 158.9 %all-gather.3.cloned.1.call-done = bf16[256,16384]{0,1:T(8,128)(2,1)} async-done(((bf16[256,256]{0,1:T(8,128)(2,1)}), bf16[256,16384]{0,1:T(8,128)(2,1)}) %all-gather.3.cloned.1.call-update) | async-done | bytes 8388624 | tf_op jit(solution)/shard_map/all_gather | solution.py:42
  167.9 12.0 %copy.17 = bf16[256,128,128]{2,0,1:T(8,128)(2,1)} copy(bf16[256,128,128]{0,2,1:T(8,128)(2,1)} %bitcast.55) | data formatting | bytes 16777216 | tf_op jit(solution)/shard_map/reshape | solution.py:43
  179.9 6.4 gather_fusion
  186.3 6.4 gather_fusion.1
  192.7 0.0 copy-start.1
  192.7 0.0 copy-start.4
  192.7 4.6 fusion.14
  197.3 0.0 copy-done.1
  197.3 0.8 copy-done.4
  198.0 0.0 copy-start.2
  198.0 1.6 fusion.19
  199.6 0.1 copy.21
  199.8 0.0 copy-done.2
  199.8 4.2 stack.11
  204.0 11.5 %all-to-all-start = ((bf16[64,256,256]{2,1,0:T(8,128)(2,1)}), bf16[64,256,256]{2,1,0:T(8,128)(2,1)}, u32[]{:S(2)}, u32[]{:S(2)}) async-start(bf16[64,256,256]{2,1,0:T(8,128)(2,1)} %stack.11), calls=%async_computation | async-start | bytes 16777216 | tf_op jit(solution)/shard_map/all_to_all | solution.py:11
  215.5 0.0 all-gather.5.cloned.1.call-start
  215.6 2.1 collective-permute-start
  217.7 1.1 collective-permute-done
  218.8 0.0 copy-start.3
  218.8 0.7 copy-done.3
  219.5 0.0 all-gather.5.cloned.1.call-update
  219.5 414.8 %all-gather.5.cloned.1.call-done = bf16[256,16384]{1,0:T(8,128)(2,1)} async-done(((bf16[256,256]{1,0:T(8,128)(2,1)}), bf16[256,16384]{1,0:T(8,128)(2,1)}) %all-gather.5.cloned.1.call-update) | async-done | bytes 8388624 | tf_op jit(solution)/shard_map/all_gather | solution.py:59
  634.3 9.2 %copy.22 = bf16[32,8,128,128]{3,2,1,0:T(8,128)(2,1)} copy(bf16[32,8,128,128]{3,1,2,0:T(8,128)(2,1)} %bitcast.54) | data formatting | bytes 16777216
  643.5 0.0 all-to-all-done
  643.5 11.4 %copy.20 = bf16[256,64,256]{2,1,0:T(8,128)(2,1)} copy(bf16[256,64,256]{2,0,1:T(8,128)(2,1)} %bitcast.12) | data formatting | bytes 16777216 | tf_op jit(solution)/shard_map/reshape | solution.py:12
  654.9 12.9 %reshape_reshape.3 = bf16[256,128,128]{2,1,0:T(8,128)(2,1)} reshape(bf16[256,64,256]{2,1,0:T(8,128)(2,1)} %copy.20) | data formatting | bytes 16777216 | tf_op jit(solution)/shard_map/reshape;reshape | solution.py:27
  667.8 0.0 copy-done
  667.8 4.6 fusion.26
  672.4 4.6 convolution_add_fusion
  677.0 0.7 fusion.24
  (4 shorter events, 0.1 us)
Async XLA Ops:
  6.5 661.3 %copy-start = (bf16[1,128,128]{2,1,0:T(8,128)(2,1)S(1)}, bf16[1,128,128]{2,1,0:T(8,128)(2,1)}, u32[]{:S(2)}) copy-start(bf16[1,128,128]{2,1,0:T(8,128)(2,1)} %param.12) | copy-start | bytes 98308
  6.5 161.4 %all-gather.3.cloned.1.call-start = ((), (), s32[]{:S(2)}) async-start(), calls=%async_computation.1 | async-start | bytes 8519680 | tf_op jit(solution)/shard_map/all_gather | solution.py:42
  192.7 4.6 copy-start.1
  192.7 5.3 copy-start.4
  198.0 1.7 copy-start.2
  204.0 439.5 %all-to-all-start = ((bf16[64,256,256]{2,1,0:T(8,128)(2,1)}), bf16[64,256,256]{2,1,0:T(8,128)(2,1)}, u32[]{:S(2)}, u32[]{:S(2)}) async-start(bf16[64,256,256]{2,1,0:T(8,128)(2,1)} %stack.11), calls=%async_computation | async-start | bytes 16777216 | tf_op jit(solution)/shard_map/all_to_all | solution.py:11
  215.5 418.8 %all-gather.5.cloned.1.call-start = ((), (), s32[]{:S(2)}) async-start(), calls=%async_computation.2 | async-start | bytes 8519680 | tf_op jit(solution)/shard_map/all_gather | solution.py:59
  215.6 3.2 collective-permute-start
  218.8 0.7 copy-start.3
Sparse Core Ops, SparseCore 0:
  10.3 157.5 all-gather.2
  219.6 414.6 all-gather.4
